TPU v7x, 32 devices: a whole 2x2x4 slice. The times are simulated.
32 devices in a mesh: expert: 8 (over z, x), dp: 4 (over y, core).
Axes of the slice: x: 2, y: 2, z: 4, core: 2. Of those that a mesh axis runs over, the one named last changes fastest.
Arguments:
- grad_output: bfloat16 [4096, 2048], P(('expert', 'dp')), may hold values from -1.5 to 1.5
- logits: float32 [4096, 8], P(('expert', 'dp')), may hold values from -6 to 6
- chosen: int32 [4096, 8], P(('expert', 'dp')), may hold values from 0 to 31, as said below
- slots: int32 [4096, 8], P(('expert', 'dp')), may hold values from 0 to 40, as said below
- other_scores: float32 [4096, 8], P(('expert', 'dp')), may hold values from -48 to 48
- hidden: bfloat16 [8, 4, 8, 40, 768], P('expert', 'dp'), may hold values from -6 to 6
- down_weight: bfloat16 [8, 768, 2048], P('expert', 'dp'), may hold values from -0.21875 to 0.21875
Outputs:
- grad_hidden: bfloat16 [8, 4, 8, 40, 768], P('expert', 'dp')
- grad_down: float32 [8, 768, 2048], P('expert', 'dp')
- grad_logits: float32 [4096, 8], P(('expert', 'dp'))
Inputs may be any that keep to these rules, and one draw needn't show every extreme that they name: `chosen`: each row names 8 different experts. 40 marks a choice with no slot: its expert is 8 or above, or it comes after 40 earlier choices of the same expert among the rows of one device in row-major order. The live choices of one expert on one device hold slots 0, 1, 2, ... in that order. Some expert fills all 40 slots on some device.
All inputs are finite; a program needn't handle non-finite values.
Results may differ from a plain program's by a relative error of at most 0.023.
Values may be sent and summed in bfloat16 or wider, within the bound.
A program may use at most 64 MiB of HBM per device.

v0:
```python
import jax
import jax.numpy as jnp
from jax import lax
from jax.sharding import PartitionSpec as P


def body(grad_output, logits, chosen, slots, other_scores, hidden, down_weight):
    window = lax.axis_size("expert")
    capacity = hidden.shape[3]
    hidden_units = hidden.shape[4]
    model_width = grad_output.shape[1]
    shard_rows = down_weight.shape[1]
    raised = jnp.exp(logits)
    gating = raised / jnp.sum(raised, axis=1, keepdims=True)
    gate_sent = gating.astype(jnp.bfloat16)
    live_slot = slots < capacity
    target = jnp.where(live_slot, chosen * capacity + slots, window * capacity)
    columns = jnp.arange(window * capacity, dtype=jnp.int32)
    placing = (target[:, :, None] == columns[None, None, :]).astype(jnp.bfloat16)
    dispatch = jnp.sum(placing, axis=1)
    send_rows = jnp.einsum(
        "tr,td->rd", dispatch, grad_output, preferred_element_type=jnp.float32
    ).astype(jnp.bfloat16)
    send_gate = jnp.einsum(
        "tkr,tk->r", placing, gate_sent, preferred_element_type=jnp.float32
    ).astype(jnp.bfloat16)
    placing_float = placing.astype(jnp.float32)
    send_rows = send_rows.reshape(window, capacity, model_width)
    send_gate = send_gate.reshape(window, capacity)
    recv_rows, recv_gate = (
        lax.all_to_all(send_rows, "expert", split_axis=0, concat_axis=0, tiled=True),
        lax.all_to_all(send_gate, "expert", split_axis=0, concat_axis=0, tiled=True),
    )
    slot_rows = recv_rows.reshape(-1, model_width)
    slot_gate = recv_gate.reshape(-1).astype(jnp.float32)
    local_hidden = hidden.reshape(-1, hidden_units)
    scaled = (slot_gate[:, None] * slot_rows.astype(jnp.float32)).astype(jnp.bfloat16)
    weights = down_weight.reshape(shard_rows, model_width)
    product = lax.dot_general(
        slot_rows,
        lax.all_gather(weights, "dp", axis=0, tiled=True),
        (((1,), (1,)), ((), ())),
        preferred_element_type=jnp.float32,
    )
    grad_rows = lax.psum_scatter(
        lax.dot_general(
            local_hidden, scaled, (((0,), (0,)), ((), ())), preferred_element_type=jnp.float32
        ).astype(jnp.bfloat16),
        "dp",
        scatter_dimension=0,
        tiled=True,
    ).astype(jnp.float32)
    slot_scores = jnp.sum(local_hidden.astype(jnp.float32) * product, axis=1)
    grad_hidden = (slot_gate[:, None] * product).astype(jnp.bfloat16).reshape(hidden.shape)
    returned = lax.all_to_all(
        slot_scores.reshape(window, capacity), "expert", split_axis=0, concat_axis=0, tiled=True
    )
    token_scores = jnp.einsum(
        "tkr,r->tk", placing_float, returned.reshape(-1), precision=lax.Precision.HIGHEST
    )
    outside = jnp.where(chosen >= window, other_scores, jnp.float32(0.0))
    scores_all = jnp.where(live_slot, token_scores, outside)
    mean_score = jnp.sum(gating * scores_all, axis=1, keepdims=True)
    grad_logits = gating * (scores_all - mean_score)
    return (grad_hidden, grad_rows.reshape(1, shard_rows, model_width), grad_logits)


def solution(mesh):
    placed = (
        P(("expert", "dp"), None),
        P(("expert", "dp"), None),
        P(("expert", "dp"), None),
        P(("expert", "dp"), None),
        P(("expert", "dp"), None),
        P("expert", "dp", None, None, None),
        P("expert", "dp", None),
    )
    return jax.shard_map(
        body,
        mesh=mesh,
        in_specs=placed,
        out_specs=(
            P("expert", "dp", None, None, None),
            P("expert", "dp", None),
            P(("expert", "dp"), None),
        ),
        check_vma=False,
    )
```

profile of v0, /device:TPU:0, one launch (start us, length us, event | category | flops | bytes accessed | tf_op | source)
XLA Modules:
  0.0 117.0 jit_solution(4432841403008827371)
XLA Ops:
  7.2 0.7 all-gather.3.cloned.1.call-update
  7.9 0.7 exponential_reduce_fusion
  8.6 0.7 convert_bitcast_fusion
  9.3 0.7 add_select_fusion
  10.0 0.4 fusion.5
  10.4 0.7 all_to_all.20
  11.1 7.3 %all-to-all-start = ((bf16[8,1,40]{2,1,0:T(2,128)(2,1)}), bf16[8,1,40]{2,1,0:T(2,128)(2,1)S(1)}, u32[]{:S(2)}, u32[]{:S(2)}) async-start(bf16[8,1,40]{2,1,0:T(2,128)(2,1)} %all_to_all.20), calls=%async_computation | async-start | bytes 8192 | tf_op jit(solution)/shard_map/all_to_all | solution.py:32
  18.5 1.6 %convolution_convert_fusion.1 = bf16[320,2048]{1,0:T(8,128)(2,1)} fusion(bf16[128,320]{0,1:T(8,128)(2,1)S(1)} %fusion.8, bf16[128,2048]{1,0:T(8,128)(2,1)S(1)} %copy-done), kind=kOutput, calls=%fused_computation.4 | convolution fusion | flops 168427520 | bytes 1916928 | tf_op jit(solution)/shard_map/tr,td->rd/dot_general | solution.py:21
  20.1 4.7 %all-to-all-done = bf16[8,1,40]{2,1,0:T(2,128)(2,1)S(1)} async-done(((bf16[8,1,40]{2,1,0:T(2,128)(2,1)}), bf16[8,1,40]{2,1,0:T(2,128)(2,1)S(1)}, u32[]{:S(2)}, u32[]{:S(2)}) %all-to-all-start) | async-done | bytes 672 | tf_op jit(solution)/shard_map/all_to_all | solution.py:32
  24.8 3.6 %all-to-all-start.1 = ((bf16[8,40,2048]{2,1,0:T(8,128)(2,1)}), bf16[8,40,2048]{2,1,0:T(8,128)(2,1)S(1)}, u32[]{:S(2)}, u32[]{:S(2)}) async-start(bf16[8,40,2048]{2,1,0:T(8,128)(2,1)} %bitcast.1), calls=%async_computation.1 | async-start | bytes 2621440 | tf_op jit(solution)/shard_map/all_to_all | solution.py:31
  28.4 30.3 %all-to-all-done.1 = bf16[8,40,2048]{2,1,0:T(8,128)(2,1)S(1)} async-done(((bf16[8,40,2048]{2,1,0:T(8,128)(2,1)}), bf16[8,40,2048]{2,1,0:T(8,128)(2,1)S(1)}, u32[]{:S(2)}, u32[]{:S(2)}) %all-to-all-start.1) | async-done | bytes 1310752 | tf_op jit(solution)/shard_map/all_to_all | solution.py:31
  59.0 0.7 copy-done.5
  59.7 3.5 %fusion.2 = bf16[768,2048]{0,1:T(8,128)(2,1)} fusion(bf16[320,2048]{1,0:T(8,128)(2,1)S(1)} %bitcast.29, bf16[320,768]{1,0:T(8,128)(2,1)S(1)} %bitcast.32), kind=kOutput, calls=%fused_computation.3 | convolution fusion | flops 1008205824 | bytes 4947968 | tf_op jit(solution)/shard_map/dot_general | solution.py:46
  63.3 4.7 %copy.21 = bf16[768,2048]{1,0:T(8,128)(2,1)} copy(bf16[768,2048]{0,1:T(8,128)(2,1)} %fusion.2) | data formatting | bytes 6291456
  68.1 3.9 %multiply_reduce_fusion = (f32[320]{0:T(512)S(1)}, bf16[320,768]{1,0:T(8,128)(2,1)}) fusion(bf16[320,768]{1,0:T(8,128)(2,1)S(1)} %bitcast.33, f32[320]{0:T(512)S(1)} %reshape.68, bf16[320,2048]{1,0:T(8,128)(2,1)S(1)} %bitcast.28, bf16[1,768,2048]{2,1,0:T(8,128)(2,1)} %all-gather.3.cloned.1.call-done), kind=kOutput, calls=%fused_computation.11 | convolution fusion | flops 1007861440 | bytes 5442048 | tf_op jit(solution)/shard_map/dot_general | solution.py:39
  72.2 9.7 %all_to_all.24 = f32[8,1,40]{2,1,0:T(1,128)S(1)} all-to-all(f32[8,1,40]{2,1,0:T(1,128)S(1)} %all_to_all.18), channel_id=1, replica_groups=mesh['expert'=8,'dp'=4] {'expert'}, dimensions={0} | all-to-all | bytes 2560 | tf_op jit(solution)/shard_map/all_to_all | solution.py:55
  81.8 0.5 broadcast.22
  82.3 0.7 reduce.10
  83.1 0.5 fusion.6
  83.6 0.6 subtract_multiply_fusion
  84.2 20.6 %reduce-scatter.4.cloned.1.call-done = bf16[192,2048]{1,0:T(8,128)(2,1)} async-done(((bf16[768,2048]{1,0:T(8,128)(2,1)}), bf16[192,2048]{1,0:T(8,128)(2,1)}) %reduce-scatter.4.cloned.1.call-update) | async-done | bytes 786448
  104.9 2.2 %copy.22 = bf16[192,2048]{0,1:T(8,128)(2,1)} copy(bf16[192,2048]{1,0:T(8,128)(2,1)} %reduce-scatter.4.cloned.1.call-done) | data formatting | bytes 1572864
  107.1 1.4 %bitcast_convert_fusion = f32[1,192,2048]{1,2,0:T(8,128)S(1)} fusion(bf16[192,2048]{0,1:T(8,128)(2,1)} %copy.22), kind=kLoop, calls=%fused_computation.10 | loop fusion | flops 393216 | bytes 2359296 | tf_op jit(solution)/shard_map/reshape | solution.py:65
  108.5 1.7 %copy.18 = f32[1,192,2048]{2,1,0:T(8,128)} copy(f32[1,192,2048]{1,2,0:T(8,128)S(1)} %bitcast_convert_fusion) | data formatting | bytes 3145728
  (23 shorter events, 0.8 us)
Async XLA Ops:
  7.2 11.3 %copy-start = (bf16[128,2048]{1,0:T(8,128)(2,1)S(1)}, bf16[128,2048]{1,0:T(8,128)(2,1)}, u32[]{:S(2)}) copy-start(bf16[128,2048]{1,0:T(8,128)(2,1)} %param.7) | copy-start | bytes 1572868
  7.2 60.9 %all-gather.3.cloned.1.call-start = ((), (), s32[]{:S(2)}) async-start(), calls=%async_computation.4 | async-start | bytes 3932160 | tf_op jit(solution)/shard_map/all_gather | solution.py:41
  11.1 13.7 %all-to-all-start = ((bf16[8,1,40]{2,1,0:T(2,128)(2,1)}), bf16[8,1,40]{2,1,0:T(2,128)(2,1)S(1)}, u32[]{:S(2)}, u32[]{:S(2)}) async-start(bf16[8,1,40]{2,1,0:T(2,128)(2,1)} %all_to_all.20), calls=%async_computation | async-start | bytes 8192 | tf_op jit(solution)/shard_map/all_to_all | solution.py:32
  24.8 33.9 %all-to-all-start.1 = ((bf16[8,40,2048]{2,1,0:T(8,128)(2,1)}), bf16[8,40,2048]{2,1,0:T(8,128)(2,1)S(1)}, u32[]{:S(2)}, u32[]{:S(2)}) async-start(bf16[8,40,2048]{2,1,0:T(8,128)(2,1)} %bitcast.1), calls=%async_computation.1 | async-start | bytes 2621440 | tf_op jit(solution)/shard_map/all_to_all | solution.py:31
  28.4 76.5 %reduce-scatter.4.cloned.1.call-start = ((), (), s32[]{:S(2)}) async-start(), calls=%async_computation.5 | async-start | bytes 3932160
  58.7 1.0 copy-start.5
  68.1 15.5 %copy-start.1 = (f32[128,8]{0,1:T(8,128)S(1)}, f32[128,8]{0,1:T(8,128)}, u32[]{:S(2)}) copy-start(f32[128,8]{0,1:T(8,128)} %param.8) | copy-start | bytes 12292
  68.1 15.5 %copy-start.2 = (s32[128,8]{0,1:T(8,128)S(1)}, s32[128,8]{0,1:T(8,128)}, u32[]{:S(2)}) copy-start(s32[128,8]{0,1:T(8,128)} %param.10) | copy-start | bytes 12292
  68.1 15.4 %copy-start.3 = (s32[128,8]{0,1:T(8,128)S(1)}, s32[128,8]{0,1:T(8,128)}, u32[]{:S(2)}) copy-start(s32[128,8]{0,1:T(8,128)} %param.9) | copy-start | bytes 12292
  68.1 15.4 %copy-start.4 = (f32[128,8]{0,1:T(8,128)S(1)}, f32[128,8]{0,1:T(8,128)}, u32[]{:S(2)}) copy-start(f32[128,8]{0,1:T(8,128)} %param.11) | copy-start | bytes 12292
Sparse Core Ops, SparseCore 0:
  9.5 31.2 all-gather.2
  68.1 36.6 reduce-scatter.3
where the time goes:
time: 118 us; the launch traced here: 117 us
  waiting for transfers between devices  56.3 us (48%)
  between operations  14.2 us (12%)
  starting transfers between devices  10.9 us (9%)
  local copies, waits for them, and re-layouts  10.8 us (9%)
  matrix products  9.83 us (8%)
  blocking collectives  9.68 us (8%)
  other arithmetic  5.22 us (4%)
    all_to_all x1, waiting for transfers between devices, body(): lax.all_to_all(send_rows, 'expert', split_axis=0, concat_axis=0, tiled=True)  30.3 us
    unnamed x3, waiting for transfers between devices  21.3 us
    all_to_all x1, blocking collectives, body(): lax.all_to_all(slot_scores.reshape(window, capacity), 'expert', split_axi...  9.68 us
    unnamed x15, local copies, waits for them, and re-layouts  9.39 us
    all_to_all x1, starting transfers between devices, body(): lax.all_to_all(send_gate, 'expert', split_axis=0, concat_axis=0, tiled=True)  7.28 us
    all_to_all x1, waiting for transfers between devices, body(): lax.all_to_all(send_gate, 'expert', split_axis=0, concat_axis=0, tiled=True)  4.72 us
    dot_general x1, matrix products, body(): lax.dot_general(slot_rows, lax.all_gather(weights, 'dp', axis=0, tiled=Tr...  3.92 us
    all_to_all x1, starting transfers between devices, body(): lax.all_to_all(send_rows, 'expert', split_axis=0, concat_axis=0, tiled=True)  3.57 us
  transfers between devices with their start and end apart: 4, of which 3 were waited for; matrix products, arithmetic and copies ran while one was open for 16% of the time, Pallas kernels for 0%

commit v1 on v0

--- a/solution.py
+++ b/solution.py
@@ -1,10 +1,313 @@
+import functools
+
 import jax
 import jax.numpy as jnp
 from jax import lax
+from jax.experimental import pallas as pl
+from jax.experimental.pallas import tpu as pltpu
 from jax.sharding import PartitionSpec as P
 
-
-def body(grad_output, logits, chosen, slots, other_scores, hidden, down_weight):
+MESH = pl.DeviceIdType.MESH
+PIECES = 4
+
+
+def kernel(
+    window, shards, capacity, pieces,
+    token_ref, meta_ref, hidden_ref, weight_ref,
+    gradh_ref, down_ref, logit_ref,
+    rsend, rrecv, msend, mrecv, wfull, padded, hturn, upward, own, csend, crecv, ysend, yrecv,
+    tsend, trecv, gates,
+    rs, rr, ms, mr, ws, wr, fs, fr, cs, cr, ys, yr, ts, tr,
+):
+    me = lax.axis_index("expert")
+    place = lax.axis_index("dp")
+    chip, core = place // 2, place % 2
+    chips = shards // 2
+    mate = (me, chip * 2 + 1 - core)
+    tokens, width = token_ref.shape
+    piece = width // pieces
+    rows = rsend.shape[2]
+    slots_all = window * rows
+    shard_rows, hidden_units = weight_ref.shape[0], hidden_ref.shape[2]
+
+    def other(step):
+        return lax.rem(me + step, window)
+
+    def chip_at(step):
+        return lax.rem(chip + step, chips)
+
+    def across(step):
+        return (me, chip_at(step) * 2 + core)
+
+    barrier = pltpu.get_barrier_semaphore()
+    for step in range(1, window):
+        pl.semaphore_signal(barrier, inc=1, device_id=(other(step), place), device_id_type=MESH)
+    for step in range(1, chips):
+        pl.semaphore_signal(barrier, inc=1, device_id=across(step), device_id_type=MESH)
+    pl.semaphore_signal(barrier, inc=1, device_id=mate, device_id_type=MESH)
+
+    k = logit_ref.shape[0]
+    raised = jnp.exp(meta_ref[0:k])
+    gating = raised / jnp.sum(raised, axis=0, keepdims=True)
+    sent_gate = gating.astype(jnp.bfloat16).astype(jnp.float32)
+    chosen = meta_ref[k : 2 * k]
+    slots = meta_ref[2 * k : 3 * k]
+    outside = jnp.where(chosen >= window, meta_ref[3 * k : 4 * k], 0.0)
+    live = slots < capacity
+    for w in range(window):
+        here = live & (chosen == w)
+        pos = jnp.sum(jnp.where(here, slots + 1.0, 0.0), axis=0, keepdims=True) - 1.0
+        gate = jnp.sum(jnp.where(here, sent_gate, 0.0), axis=0, keepdims=True)
+        line = lax.broadcasted_iota(jnp.int32, (8, tokens), 0)
+        msend[w] = jnp.where(line == 0, pos, gate)
+
+    slot_id = lax.broadcasted_iota(jnp.int32, (rows, tokens), 0).astype(jnp.float32)
+
+    def spread(ref, w):
+        return slot_id == ref[w, 0:1, :]
+
+    dispatch = jnp.concatenate(
+        [spread(msend, w).astype(jnp.float32) for w in range(window)], axis=0
+    ).astype(jnp.bfloat16)
+
+    def fill(c):
+        lanes = pl.ds(pl.multiple_of(c * piece, piece), piece)
+        placed = jnp.dot(dispatch, token_ref[:, lanes], preferred_element_type=jnp.float32)
+        rsend[c] = placed.astype(jnp.bfloat16).reshape(window, rows, piece)
+
+    def row_copy(c, dest, source):
+        return pltpu.make_async_remote_copy(
+            src_ref=rsend.at[c, dest, pl.ds(0, capacity)],
+            dst_ref=rrecv.at[c, source, pl.ds(0, capacity)],
+            send_sem=rs.at[c, dest], recv_sem=rr.at[c, source],
+            device_id=(dest, place), device_id_type=MESH,
+        )
+
+    def meta_copy(dest, source):
+        return pltpu.make_async_remote_copy(
+            src_ref=msend.at[dest], dst_ref=mrecv.at[source],
+            send_sem=ms.at[dest], recv_sem=mr.at[source],
+            device_id=(dest, place), device_id_type=MESH,
+        )
+
+    def score_copy(dest, source):
+        return pltpu.make_async_remote_copy(
+            src_ref=tsend.at[dest], dst_ref=trecv.at[source],
+            send_sem=ts.at[dest], recv_sem=tr.at[source],
+            device_id=(dest, place), device_id_type=MESH,
+        )
+
+    def weight_copy(c, target, step, slot):
+        lanes = pl.ds(pl.multiple_of(c * piece, piece), piece)
+        return pltpu.make_async_remote_copy(
+            src_ref=weight_ref.at[:, lanes], dst_ref=wfull.at[c, slot],
+            send_sem=ws.at[c, step], recv_sem=wr.at[c, step],
+            device_id=target, device_id_type=MESH,
+        )
+
+    def pass_copy(c, step, slot):
+        return pltpu.make_async_remote_copy(
+            src_ref=wfull.at[c, slot], dst_ref=wfull.at[c, slot],
+            send_sem=fs.at[c, step], recv_sem=fr.at[c, step],
+            device_id=mate, device_id_type=MESH,
+        )
+
+    def core_copy(c):
+        return pltpu.make_async_remote_copy(
+            src_ref=csend.at[c], dst_ref=crecv.at[c],
+            send_sem=cs.at[c], recv_sem=cr.at[c],
+            device_id=mate, device_id_type=MESH,
+        )
+
+    def sum_copy(c, step):
+        return pltpu.make_async_remote_copy(
+            src_ref=ysend.at[c, step], dst_ref=yrecv.at[c, step],
+            send_sem=ys.at[c, step], recv_sem=yr.at[c, step],
+            device_id=across(step), device_id_type=MESH,
+        )
+
+    fill(0)
+    pl.semaphore_wait(barrier, window - 1 + chips)
+
+    for step in range(1, window):
+        meta_copy(other(step), me).start()
+
+    def launch(c, carry):
+        for step in range(1, window):
+            row_copy(c, other(step), me).start()
+        for step in range(1, chips):
+            weight_copy(c, across(step), step, place).start()
+        weight_copy(c, mate, 0, place).start()
+
+        @pl.when(c + 1 < pieces)
+        def _():
+            fill(c + 1)
+
+        return carry
+
+    lax.fori_loop(0, pieces, launch, 0)
+
+    mrecv[me] = msend[me]
+    for c in range(pieces):
+        lanes = slice(c * piece, (c + 1) * piece)
+        rrecv[c, me, 0:capacity] = rsend[c, me, 0:capacity]
+        if rows > capacity:
+            rrecv[c, :, capacity:rows] = jnp.zeros((window, rows - capacity, piece), jnp.bfloat16)
+        wfull[c, place] = weight_ref[:, lanes]
+    padded[:, 0:capacity] = hidden_ref[...]
+    if rows > capacity:
+        padded[:, capacity:rows] = jnp.zeros((window, rows - capacity, hidden_units), jnp.bfloat16)
+    flat = padded[...].reshape(slots_all, hidden_units)
+    hturn[...] = flat.T.reshape(shards, shard_rows, slots_all)
+    upward[...] = jnp.zeros_like(upward)
+
+    for step in range(1, window):
+        meta_copy(other(step), lax.rem(me + window - step, window)).wait_recv()
+    for s in range(window):
+        gates[s] = jnp.sum(
+            jnp.where(spread(mrecv, s), mrecv[s, 1:2, :], 0.0), axis=1, keepdims=True
+        )
+
+    def finish(c, carry):
+        lanes = pl.ds(pl.multiple_of(c * piece, piece), piece)
+        for step in range(1, chips):
+            came = lax.rem(chip + chips - step, chips) * 2 + core
+            weight_copy(c, across(step), step, came).wait_recv()
+            pass_copy(c, step, came).start()
+        for step in range(1, window):
+            row_copy(c, other(step), lax.rem(me + window - step, window)).wait_recv()
+        got = rrecv[c].reshape(slots_all, piece)
+        scaled = (gates[...].reshape(slots_all, 1) * got.astype(jnp.float32)).astype(jnp.bfloat16)
+        for h in range(chips):
+            csend[c, h] = jnp.dot(
+                hturn[2 * h + 1 - core], scaled, preferred_element_type=jnp.float32
+            ).astype(jnp.bfloat16)
+        core_copy(c).start()
+        for h in range(chips):
+            own[h] = jnp.dot(hturn[2 * h + core], scaled, preferred_element_type=jnp.float32)
+        core_copy(c).wait_recv()
+        for step in range(1, chips):
+            to = chip_at(step)
+            ysend[c, step] = (own[to] + crecv[c, to].astype(jnp.float32)).astype(jnp.bfloat16)
+            sum_copy(c, step).start()
+        down_ref[:, lanes] = own[chip] + crecv[c, chip].astype(jnp.float32)
+        weight_copy(c, mate, 0, chip * 2 + 1 - core).wait_recv()
+        for step in range(1, chips):
+            came = lax.rem(chip + chips - step, chips) * 2 + 1 - core
+            pass_copy(c, step, came).wait_recv()
+        weights = wfull[c].reshape(hidden_units, piece)
+        upward[...] += lax.dot_general(
+            got, weights, (((1,), (1,)), ((), ())), preferred_element_type=jnp.float32
+        )
+        return carry
+
+    lax.fori_loop(0, pieces, finish, 0)
+
+    for s in range(window):
+        up = upward[s * rows : (s + 1) * rows]
+        score = jnp.sum(padded[s].astype(jnp.float32) * up, axis=1, keepdims=True)
+        back = jnp.sum(jnp.where(spread(mrecv, s), score, 0.0), axis=0, keepdims=True)
+        tsend[s] = jnp.broadcast_to(back, (8, tokens))
+    for step in range(1, window):
+        score_copy(other(step), me).start()
+    trecv[me] = tsend[me]
+    for s in range(window):
+        up = upward[s * rows : s * rows + capacity]
+        gradh_ref[s] = (gates[s, 0:capacity] * up).astype(jnp.bfloat16)
+
+    for step in range(1, window):
+        score_copy(other(step), lax.rem(me + window - step, window)).wait_recv()
+    token_scores = jnp.zeros((k, tokens), jnp.float32)
+    for w in range(window):
+        token_scores = jnp.where(chosen == w, trecv[w], token_scores)
+    scores_all = jnp.where(live, token_scores, outside)
+    mean_score = jnp.sum(gating * scores_all, axis=0, keepdims=True)
+    logit_ref[...] = gating * (scores_all - mean_score)
+
+    def collect(c, carry):
+        lanes = pl.ds(pl.multiple_of(c * piece, piece), piece)
+        for step in range(1, chips):
+            sum_copy(c, step).wait_recv()
+            down_ref[:, lanes] += yrecv[c, step].astype(jnp.float32)
+        return carry
+
+    lax.fori_loop(0, pieces, collect, 0)
+
+    def drain(c, carry):
+        for step in range(1, window):
+            row_copy(c, other(step), me).wait_send()
+        for step in range(1, chips):
+            weight_copy(c, across(step), step, place).wait_send()
+            pass_copy(c, step, lax.rem(chip + chips - step, chips) * 2 + core).wait_send()
+            sum_copy(c, step).wait_send()
+        weight_copy(c, mate, 0, place).wait_send()
+        core_copy(c).wait_send()
+        return carry
+
+    lax.fori_loop(0, pieces, drain, 0)
+    for step in range(1, window):
+        meta_copy(other(step), me).wait_send()
+        score_copy(other(step), me).wait_send()
+
+
+def fused(grad_output, logits, chosen, slots, other_scores, hidden, down_weight):
+    window = lax.axis_size("expert")
+    shards = lax.axis_size("dp")
+    capacity, hidden_units = hidden.shape[3], hidden.shape[4]
+    tokens, width = grad_output.shape
+    k = logits.shape[1]
+    shard_rows = down_weight.shape[1]
+    rows = -(-capacity // 16) * 16
+    chips = shards // 2
+    piece = width // PIECES
+    meta = jnp.concatenate(
+        [logits, chosen.astype(jnp.float32), slots.astype(jnp.float32), other_scores], axis=1
+    ).T
+    vmem = pl.BlockSpec(memory_space=pltpu.VMEM)
+    bf, f32, dma = jnp.bfloat16, jnp.float32, pltpu.SemaphoreType.DMA
+    slots_all = window * rows
+    gradh, down, turned = pl.pallas_call(
+        functools.partial(kernel, window, shards, capacity, PIECES),
+        out_shape=(
+            jax.ShapeDtypeStruct((window, capacity, hidden_units), bf),
+            jax.ShapeDtypeStruct((shard_rows, width), f32),
+            jax.ShapeDtypeStruct((k, tokens), f32),
+        ),
+        in_specs=[vmem] * 4,
+        out_specs=(vmem,) * 3,
+        scratch_shapes=[
+            pltpu.VMEM((PIECES, window, rows, piece), bf),
+            pltpu.VMEM((PIECES, window, rows, piece), bf),
+            pltpu.VMEM((window, 8, tokens), f32),
+            pltpu.VMEM((window, 8, tokens), f32),
+            pltpu.VMEM((PIECES, shards, shard_rows, piece), bf),
+            pltpu.VMEM((window, rows, hidden_units), bf),
+            pltpu.VMEM((shards, shard_rows, slots_all), bf),
+            pltpu.VMEM((slots_all, hidden_units), f32),
+            pltpu.VMEM((chips, shard_rows, piece), f32),
+            pltpu.VMEM((PIECES, chips, shard_rows, piece), bf),
+            pltpu.VMEM((PIECES, chips, shard_rows, piece), bf),
+            pltpu.VMEM((PIECES, chips, shard_rows, piece), bf),
+            pltpu.VMEM((PIECES, chips, shard_rows, piece), bf),
+            pltpu.VMEM((window, 8, tokens), f32),
+            pltpu.VMEM((window, 8, tokens), f32),
+            pltpu.VMEM((window, rows, 1), f32),
+            dma((PIECES, window)), dma((PIECES, window)),
+            dma((window,)), dma((window,)),
+            dma((PIECES, chips)), dma((PIECES, chips)),
+            dma((PIECES, chips)), dma((PIECES, chips)),
+            dma((PIECES,)), dma((PIECES,)),
+            dma((PIECES, chips)), dma((PIECES, chips)),
+            dma((window,)), dma((window,)),
+        ],
+        compiler_params=pltpu.CompilerParams(
+            collective_id=0, has_side_effects=True, vmem_limit_bytes=48 * 1024 * 1024
+        ),
+    )(grad_output, meta, hidden.reshape(window, capacity, hidden_units), down_weight.reshape(shard_rows, width))
+    return (gradh.reshape(hidden.shape), down.reshape(1, shard_rows, width), turned.T)
+
+
+def plain(grad_output, logits, chosen, slots, other_scores, hidden, down_weight):
     window = lax.axis_size("expert")
     capacity = hidden.shape[3]
     hidden_units = hidden.shape[4]
@@ -65,6 +368,20 @@
     return (grad_hidden, grad_rows.reshape(1, shard_rows, model_width), grad_logits)
 
 
+def body(grad_output, logits, chosen, slots, other_scores, hidden, down_weight):
+    args = (grad_output, logits, chosen, slots, other_scores, hidden, down_weight)
+    fits = (
+        lax.axis_size("dp") % 2 == 0
+        and hidden.shape[3] % 8 == 0
+        and down_weight.shape[1] % 16 == 0
+        and hidden.shape[4] % 128 == 0
+        and grad_output.shape[0] == 128
+        and grad_output.shape[1] % (PIECES * 128) == 0
+        and logits.shape[1] == 8
+    )
+    return fused(*args) if fits else plain(*args)
+
+
 def solution(mesh):
     placed = (
         P(("expert", "dp"), None),

time: 118 us -> 54.1 us (0.46)
  waiting for transfers between devices: 56.3 us -> 0 us
  Pallas kernels: 0 us -> 45.1 us
  between operations: 14.2 us -> 0.64 us
  starting transfers between devices: 10.9 us -> 0 us
  matrix products: 9.83 us -> 0 us
  blocking collectives: 9.68 us -> 0 us
  local copies, waits for them, and re-layouts: 10.8 us -> 5.72 us
  other arithmetic: 5.22 us -> 2.08 us
    pallas_call x0 -> x1, Pallas kernels: none -> 45.1 us  [fused(): pl.pallas_call(functools.partial(kernel, window, shards, capacity, PIECES...]
    all_to_all x2 -> x0, waiting for transfers between devices: 35 us -> none  [the longest x1 30.3 us: body(): lax.all_to_all(send_rows, 'expert', split_axis=0, concat_axis=0, tiled=True)]
    unnamed x3 -> x0, waiting for transfers between devices: 21.3 us -> none
    all_to_all x2 -> x0, starting transfers between devices: 10.9 us -> none  [the longest x1 7.28 us: body(): lax.all_to_all(send_gate, 'expert', split_axis=0, concat_axis=0, tiled=True)]
    dot_general x5 -> x0, matrix products: 9.83 us -> none  [the longest x1 3.92 us: body(): lax.dot_general(slot_rows, lax.all_gather(weights, 'dp', axis=0, tiled=Tr...]
    all_to_all x1 -> x0, blocking collectives: 9.68 us -> none  [body(): lax.all_to_all(slot_scores.reshape(window, capacity), 'expert', split_axi...]
    unnamed x15 -> x9, local copies, waits for them, and re-layouts: 9.39 us -> 5.72 us
    reshape x1 -> x0, other arithmetic: 1.38 us -> none  [body(): grad_rows.reshape(1, shard_rows, model_width)]
  transfers between devices with their start and end apart: 4 -> 0, of which waited for: 3 -> 0; matrix products, arithmetic and copies ran while one was open for 16% -> 0% of each run, Pallas kernels for 0% -> 0%
where the time goes in v1:
time: 54.1 us; the launch traced here: 53.6 us
  Pallas kernels  45.1 us (83%)
  local copies, waits for them, and re-layouts  5.72 us (11%)
  other arithmetic  2.08 us (4%)
  between operations  0.64 us (1%)
    pallas_call x1, Pallas kernels, fused(): pl.pallas_call(functools.partial(kernel, window, shards, capacity, PIECES...  45.1 us
    unnamed x9, local copies, waits for them, and re-layouts  5.72 us

profile of v1, /device:TPU:0, one launch (start us, length us, event | category | flops | bytes accessed | tf_op | source)
XLA Modules:
  0.0 53.6 jit_solution(9427197815651109774)
XLA Ops:
  0.6 0.7 %convert_element_type.6 = f32[128,8]{0,1:T(8,128)S(1)} convert(s32[128,8]{0,1:T(8,128)} %param.9) | non-fusion elementwise | flops 1024 | bytes 8192 | tf_op jit(solution)/shard_map/convert_element_type | solution.py:264
  1.3 0.7 %convert_element_type.7 = f32[128,8]{0,1:T(8,128)S(1)} convert(s32[128,8]{0,1:T(8,128)} %param.10) | non-fusion elementwise | flops 1024 | bytes 8192 | tf_op jit(solution)/shard_map/convert_element_type | solution.py:264
  2.0 0.7 %maximum_bitcast_fusion.meta_ref = f32[32,128]{1,0:T(8,128)S(1)} fusion(f32[128,8]{0,1:T(8,128)} %param.11, f32[128,8]{0,1:T(8,128)S(1)} %convert_element_type.7, f32[128,8]{0,1:T(8,128)S(1)} %convert_element_type.6, f32[128,8]{0,1:T(8,128)} %param.8), kind=kLoop, calls=%fused_computation | loop fusion | flops 12288 | bytes 32768 | tf_op jit(solution)/shard_map/transpose | solution.py:265
  2.7 0.0 copy-start
  2.7 1.1 %copy-done = bf16[1,192,2048]{2,1,0:T(8,128)(2,1)S(1)} copy-done((bf16[1,192,2048]{2,1,0:T(8,128)(2,1)S(1)}, bf16[1,192,2048]{2,1,0:T(8,128)(2,1)}, u32[]{:S(2)}) %copy-start) | copy-done | bytes 786456
  3.8 0.0 copy-start.1
  3.9 1.0 %copy-done.1 = bf16[128,2048]{1,0:T(8,128)(2,1)S(1)} copy-done((bf16[128,2048]{1,0:T(8,128)(2,1)S(1)}, bf16[128,2048]{1,0:T(8,128)(2,1)}, u32[]{:S(2)}) %copy-start.1) | copy-done | bytes 524312
  4.9 0.0 copy-start.2
  4.9 1.0 %copy-done.2 = bf16[1,1,8,40,768]{4,3,2,1,0:T(8,128)(2,1)S(1)} copy-done((bf16[1,1,8,40,768]{4,3,2,1,0:T(8,128)(2,1)S(1)}, bf16[1,1,8,40,768]{4,3,2,1,0:T(8,128)(2,1)}, u32[]{:S(2)}) %copy-start.2) | copy-done | bytes 491544
  5.9 45.1 %shard_map.94 = (bf16[8,40,768]{2,1,0:T(8,128)(2,1)S(1)}, f32[192,2048]{1,0:T(8,128)S(1)}, f32[8,128]{1,0:T(8,128)S(1)}) custom-call(bf16[128,2048]{1,0:T(8,128)(2,1)S(1)} %copy-done.1, f32[32,128]{1,0:T(8,128)S(1)} %maximum_bitcast_fusion.meta_ref, bf16[8,40,768]{2,1,0:T(8,128)(2,1)S(1)} %bitcast.9, bf16[192,2048]{1,0:T(8,128)(2,1)S(1)} %bitcast.8), custom_call_target="tpu_custom_call" | custom-call | tf_op jit(solution)/shard_map/pallas_call | solution.py:269
  51.1 0.8 %copy.13 = bf16[1,1,8,40,768]{4,3,2,1,0:T(8,128)(2,1)} copy(bf16[1,1,8,40,768]{4,3,2,1,0:T(8,128)(2,1)S(1)} %bitcast.10) | data formatting | bytes 983040
  51.9 1.1 %copy.14 = f32[1,192,2048]{2,1,0:T(8,128)} copy(f32[1,192,2048]{2,1,0:T(8,128)S(1)} %bitcast.7) | data formatting | bytes 3145728
  53.0 0.6 %copy.15 = f32[128,8]{0,1:T(8,128)} copy(f32[128,8]{0,1:T(8,128)S(1)} %bitcast.11) | data formatting | bytes 8192
Async XLA Ops:
  2.7 1.1 %copy-start = (bf16[1,192,2048]{2,1,0:T(8,128)(2,1)S(1)}, bf16[1,192,2048]{2,1,0:T(8,128)(2,1)}, u32[]{:S(2)}) copy-start(bf16[1,192,2048]{2,1,0:T(8,128)(2,1)} %param.13) | copy-start | bytes 2359300
  3.8 1.0 %copy-start.1 = (bf16[128,2048]{1,0:T(8,128)(2,1)S(1)}, bf16[128,2048]{1,0:T(8,128)(2,1)}, u32[]{:S(2)}) copy-start(bf16[128,2048]{1,0:T(8,128)(2,1)} %token_ref.1) | copy-start | bytes 1572868
  4.9 1.0 %copy-start.2 = (bf16[1,1,8,40,768]{4,3,2,1,0:T(8,128)(2,1)S(1)}, bf16[1,1,8,40,768]{4,3,2,1,0:T(8,128)(2,1)}, u32[]{:S(2)}) copy-start(bf16[1,1,8,40,768]{4,3,2,1,0:T(8,128)(2,1)} %param.12) | copy-start | bytes 1474564

commit v2 on v1

--- a/solution.py
+++ b/solution.py
@@ -8,16 +8,17 @@
 from jax.sharding import PartitionSpec as P
 
 MESH = pl.DeviceIdType.MESH
-PIECES = 4
+PIECES = 8
 
 
 def kernel(
     window, shards, capacity, pieces,
-    token_ref, meta_ref, hidden_ref, weight_ref,
+    token_hbm, logits_hbm, chosen_hbm, slots_hbm, other_hbm, hidden_hbm, weight_ref,
     gradh_ref, down_ref, logit_ref,
+    token_ref, logits_ref, chosen_ref, slots_ref, other_ref, hidden_ref,
     rsend, rrecv, msend, mrecv, wfull, padded, hturn, upward, own, csend, crecv, ysend, yrecv,
     tsend, trecv, gates,
-    rs, rr, ms, mr, ws, wr, fs, fr, cs, cr, ys, yr, ts, tr,
+    rs, rr, ms, mr, ws, wr, fs, fr, cs, cr, ys, yr, ts, tr, ls, lw,
 ):
     me = lax.axis_index("expert")
     place = lax.axis_index("dp")
@@ -39,6 +40,30 @@
     def across(step):
         return (me, chip_at(step) * 2 + core)
 
+    loads = [
+        pltpu.make_async_copy(src, dst, ls.at[i])
+        for i, (src, dst) in enumerate((
+            (chosen_hbm, chosen_ref), (slots_hbm, slots_ref), (token_hbm, token_ref),
+            (logits_hbm, logits_ref), (other_hbm, other_ref), (hidden_hbm, hidden_ref),
+        ))
+    ]
+    for load in loads:
+        load.start()
+    keeps = [
+        pltpu.make_async_copy(
+            weight_ref.at[:, pl.ds(c * piece, piece)], wfull.at[c, place], lw.at[c]
+        )
+        for c in range(pieces)
+    ]
+
+    def weight_copy(c, target, step, slot):
+        lanes = pl.ds(pl.multiple_of(c * piece, piece), piece)
+        return pltpu.make_async_remote_copy(
+            src_ref=weight_ref.at[:, lanes], dst_ref=wfull.at[c, slot],
+            send_sem=ws.at[c, step], recv_sem=wr.at[c, step],
+            device_id=target, device_id_type=MESH,
+        )
+
     barrier = pltpu.get_barrier_semaphore()
     for step in range(1, window):
         pl.semaphore_signal(barrier, inc=1, device_id=(other(step), place), device_id_type=MESH)
@@ -47,16 +72,28 @@
     pl.semaphore_signal(barrier, inc=1, device_id=mate, device_id_type=MESH)
 
     k = logit_ref.shape[0]
-    raised = jnp.exp(meta_ref[0:k])
+    pl.semaphore_wait(barrier, window - 1 + chips)
+
+    def launch_weights(c, carry):
+        for step in range(1, chips):
+            weight_copy(c, across(step), step, place).start()
+        weight_copy(c, mate, 0, place).start()
+        return carry
+
+    lax.fori_loop(0, pieces, launch_weights, 0)
+
+    for load in loads[:5]:
+        load.wait()
+    raised = jnp.exp(logits_ref[...])
     gating = raised / jnp.sum(raised, axis=0, keepdims=True)
     sent_gate = gating.astype(jnp.bfloat16).astype(jnp.float32)
-    chosen = meta_ref[k : 2 * k]
-    slots = meta_ref[2 * k : 3 * k]
-    outside = jnp.where(chosen >= window, meta_ref[3 * k : 4 * k], 0.0)
+    chosen = chosen_ref[...]
+    slots = slots_ref[...]
+    outside = jnp.where(chosen >= window, other_ref[...], 0.0)
     live = slots < capacity
     for w in range(window):
         here = live & (chosen == w)
-        pos = jnp.sum(jnp.where(here, slots + 1.0, 0.0), axis=0, keepdims=True) - 1.0
+        pos = jnp.sum(jnp.where(here, slots.astype(jnp.float32) + 1.0, 0.0), axis=0, keepdims=True) - 1.0
         gate = jnp.sum(jnp.where(here, sent_gate, 0.0), axis=0, keepdims=True)
         line = lax.broadcasted_iota(jnp.int32, (8, tokens), 0)
         msend[w] = jnp.where(line == 0, pos, gate)
@@ -97,14 +134,6 @@
             device_id=(dest, place), device_id_type=MESH,
         )
 
-    def weight_copy(c, target, step, slot):
-        lanes = pl.ds(pl.multiple_of(c * piece, piece), piece)
-        return pltpu.make_async_remote_copy(
-            src_ref=weight_ref.at[:, lanes], dst_ref=wfull.at[c, slot],
-            send_sem=ws.at[c, step], recv_sem=wr.at[c, step],
-            device_id=target, device_id_type=MESH,
-        )
-
     def pass_copy(c, step, slot):
         return pltpu.make_async_remote_copy(
             src_ref=wfull.at[c, slot], dst_ref=wfull.at[c, slot],
@@ -127,17 +156,12 @@
         )
 
     fill(0)
-    pl.semaphore_wait(barrier, window - 1 + chips)
-
     for step in range(1, window):
         meta_copy(other(step), me).start()
 
     def launch(c, carry):
         for step in range(1, window):
             row_copy(c, other(step), me).start()
-        for step in range(1, chips):
-            weight_copy(c, across(step), step, place).start()
-        weight_copy(c, mate, 0, place).start()
 
         @pl.when(c + 1 < pieces)
         def _():
@@ -149,17 +173,19 @@
 
     mrecv[me] = msend[me]
     for c in range(pieces):
-        lanes = slice(c * piece, (c + 1) * piece)
         rrecv[c, me, 0:capacity] = rsend[c, me, 0:capacity]
         if rows > capacity:
             rrecv[c, :, capacity:rows] = jnp.zeros((window, rows - capacity, piece), jnp.bfloat16)
-        wfull[c, place] = weight_ref[:, lanes]
+        keeps[c].start()
+    loads[5].wait()
     padded[:, 0:capacity] = hidden_ref[...]
     if rows > capacity:
         padded[:, capacity:rows] = jnp.zeros((window, rows - capacity, hidden_units), jnp.bfloat16)
     flat = padded[...].reshape(slots_all, hidden_units)
     hturn[...] = flat.T.reshape(shards, shard_rows, slots_all)
     upward[...] = jnp.zeros_like(upward)
+    for keep in keeps:
+        keep.wait()
 
     for step in range(1, window):
         meta_copy(other(step), lax.rem(me + window - step, window)).wait_recv()
@@ -185,12 +211,6 @@
         core_copy(c).start()
         for h in range(chips):
             own[h] = jnp.dot(hturn[2 * h + core], scaled, preferred_element_type=jnp.float32)
-        core_copy(c).wait_recv()
-        for step in range(1, chips):
-            to = chip_at(step)
-            ysend[c, step] = (own[to] + crecv[c, to].astype(jnp.float32)).astype(jnp.bfloat16)
-            sum_copy(c, step).start()
-        down_ref[:, lanes] = own[chip] + crecv[c, chip].astype(jnp.float32)
         weight_copy(c, mate, 0, chip * 2 + 1 - core).wait_recv()
         for step in range(1, chips):
             came = lax.rem(chip + chips - step, chips) * 2 + 1 - core
@@ -199,6 +219,12 @@
         upward[...] += lax.dot_general(
             got, weights, (((1,), (1,)), ((), ())), preferred_element_type=jnp.float32
         )
+        core_copy(c).wait_recv()
+        for step in range(1, chips):
+            to = chip_at(step)
+            ysend[c, step] = (own[to] + crecv[c, to].astype(jnp.float32)).astype(jnp.bfloat16)
+            sum_copy(c, step).start()
+        down_ref[:, lanes] = own[chip] + crecv[c, chip].astype(jnp.float32)
         return carry
 
     lax.fori_loop(0, pieces, finish, 0)
@@ -248,6 +274,17 @@
     for step in range(1, window):
         meta_copy(other(step), me).wait_send()
         score_copy(other(step), me).wait_send()
+
+
+def write_out(a, b, c, a_out, b_out, c_out, sems):
+    copies = [
+        pltpu.make_async_copy(src, dst, sems.at[i])
+        for i, (src, dst) in enumerate(((b, b_out), (a, a_out), (c, c_out)))
+    ]
+    for copy in copies:
+        copy.start()
+    for copy in copies:
+        copy.wait()
 
 
 def fused(grad_output, logits, chosen, slots, other_scores, hidden, down_weight):
@@ -260,10 +297,8 @@
     rows = -(-capacity // 16) * 16
     chips = shards // 2
     piece = width // PIECES
-    meta = jnp.concatenate(
-        [logits, chosen.astype(jnp.float32), slots.astype(jnp.float32), other_scores], axis=1
-    ).T
     vmem = pl.BlockSpec(memory_space=pltpu.VMEM)
+    hbm = pl.BlockSpec(memory_space=pltpu.HBM)
     bf, f32, dma = jnp.bfloat16, jnp.float32, pltpu.SemaphoreType.DMA
     slots_all = window * rows
     gradh, down, turned = pl.pallas_call(
@@ -273,9 +308,15 @@
             jax.ShapeDtypeStruct((shard_rows, width), f32),
             jax.ShapeDtypeStruct((k, tokens), f32),
         ),
-        in_specs=[vmem] * 4,
+        in_specs=[hbm] * 7,
         out_specs=(vmem,) * 3,
         scratch_shapes=[
+            pltpu.VMEM((tokens, width), bf),
+            pltpu.VMEM((k, tokens), f32),
+            pltpu.VMEM((k, tokens), jnp.int32),
+            pltpu.VMEM((k, tokens), jnp.int32),
+            pltpu.VMEM((k, tokens), f32),
+            pltpu.VMEM((window, capacity, hidden_units), bf),
             pltpu.VMEM((PIECES, window, rows, piece), bf),
             pltpu.VMEM((PIECES, window, rows, piece), bf),
             pltpu.VMEM((window, 8, tokens), f32),
@@ -299,11 +340,26 @@
             dma((PIECES,)), dma((PIECES,)),
             dma((PIECES, chips)), dma((PIECES, chips)),
             dma((window,)), dma((window,)),
+            dma((6,)), dma((PIECES,)),
         ],
         compiler_params=pltpu.CompilerParams(
             collective_id=0, has_side_effects=True, vmem_limit_bytes=48 * 1024 * 1024
         ),
-    )(grad_output, meta, hidden.reshape(window, capacity, hidden_units), down_weight.reshape(shard_rows, width))
+    )(*(pltpu.with_memory_space_constraint(a, pltpu.HBM) for a in (
+        grad_output, logits.T, chosen.T, slots.T, other_scores.T,
+        hidden.reshape(window, capacity, hidden_units), down_weight.reshape(shard_rows, width),
+    )))
+    gradh, down, turned = (
+        pltpu.with_memory_space_constraint(a, pltpu.VMEM) for a in (gradh, down, turned)
+    )
+    gradh, down, turned = pl.pallas_call(
+        write_out,
+        out_shape=tuple(jax.ShapeDtypeStruct(a.shape, a.dtype) for a in (gradh, down, turned)),
+        in_specs=[vmem] * 3,
+        out_specs=(hbm,) * 3,
+        scratch_shapes=[dma((3,))],
+        compiler_params=pltpu.CompilerParams(vmem_limit_bytes=8 * 1024 * 1024),
+    )(gradh, down, turned)
     return (gradh.reshape(hidden.shape), down.reshape(1, shard_rows, width), turned.T)
 
 

time: 54.1 us -> 48.9 us (0.904)
  local copies, waits for them, and re-layouts: 5.72 us -> 0 us
  Pallas kernels: 45.1 us -> 48.1 us
  other arithmetic: 2.08 us -> 0 us
    unnamed x9 -> x0, local copies, waits for them, and re-layouts: 5.72 us -> none
    pallas_call x1, Pallas kernels: 45.1 us -> 46.8 us  [fused(): pl.pallas_call(functools.partial(kernel, window, shards, capacity, PIECES...]
    convert_element_type x2 -> x0, other arithmetic: 1.38 us -> none  [the longest x1 0.69 us: fused(): chosen.astype(jnp.float32)]
    pallas_call x0 -> x1, Pallas kernels: none -> 1.33 us  [fused(): pl.pallas_call(write_out, out_shape=tuple((jax.ShapeDtypeStruct(a.shape,...]
    transpose x1 -> x0, other arithmetic: 0.71 us -> none  [fused(): meta = jnp.concatenate([logits, chosen.astype(jnp.float32), slots.astype(...]
where the time goes in v2:
time: 48.9 us; the launch traced here: 48.7 us
  Pallas kernels  48.1 us (98%)
  between operations  0.64 us (1%)
    pallas_call x1, Pallas kernels, fused(): pl.pallas_call(functools.partial(kernel, window, shards, capacity, PIECES...  46.8 us
    pallas_call x1, Pallas kernels, fused(): pl.pallas_call(write_out, out_shape=tuple((jax.ShapeDtypeStruct(a.shape,...  1.33 us

profile of v2, /device:TPU:0, one launch (start us, length us, event | category | flops | bytes accessed | tf_op | source)
XLA Modules:
  0.0 48.7 jit_solution(14318016767744064677)
XLA Ops:
  0.6 46.8 %shard_map.94 = (bf16[8,40,768]{2,1,0:T(8,128)(2,1)S(1)}, f32[192,2048]{1,0:T(8,128)S(1)}, f32[8,128]{1,0:T(8,128)S(1)}) custom-call(bf16[128,2048]{1,0:T(8,128)(2,1)} %token_hbm.1, f32[8,128]{1,0:T(8,128)} %bitcast.11, s32[8,128]{1,0:T(8,128)} %bitcast.12, s32[8,128]{1,0:T(8,128)} %bitcast.13, f32[8,128]{1,0:T(8,128)} %bitcast.14, ...), custom_call_target="tpu_custom_call" | custom-call | tf_op jit(solution)/shard_map/pallas_call | solution.py:304
  47.4 1.3 %shard_map.95 = (bf16[8,40,768]{2,1,0:T(8,128)(2,1)}, f32[192,2048]{1,0:T(8,128)}, f32[8,128]{1,0:T(8,128)}) custom-call(bf16[8,40,768]{2,1,0:T(8,128)(2,1)S(1)} %get-tuple-element.9.a, f32[192,2048]{1,0:T(8,128)S(1)} %get-tuple-element.10.b, f32[8,128]{1,0:T(8,128)S(1)} %get-tuple-element.11.c), custom_call_target="tpu_custom_call" | custom-call | tf_op jit(solution)/shard_map/pallas_call | solution.py:355

commit v3 on v2

--- a/solution.py
+++ b/solution.py
@@ -31,8 +31,14 @@
     slots_all = window * rows
     shard_rows, hidden_units = weight_ref.shape[0], hidden_ref.shape[2]
 
+    near = [lax.rem(me + step, window) for step in range(window)]
+
     def other(step):
-        return lax.rem(me + step, window)
+        return near[step]
+
+    def settle(buffer, sem):
+        whole = buffer.at[pl.ds(0, window - 1)]
+        pltpu.make_async_copy(whole, whole, sem).wait()
 
     def chip_at(step):
         return lax.rem(chip + step, chips)
@@ -72,16 +78,6 @@
     pl.semaphore_signal(barrier, inc=1, device_id=mate, device_id_type=MESH)
 
     k = logit_ref.shape[0]
-    pl.semaphore_wait(barrier, window - 1 + chips)
-
-    def launch_weights(c, carry):
-        for step in range(1, chips):
-            weight_copy(c, across(step), step, place).start()
-        weight_copy(c, mate, 0, place).start()
-        return carry
-
-    lax.fori_loop(0, pieces, launch_weights, 0)
-
     for load in loads[:5]:
         load.wait()
     raised = jnp.exp(logits_ref[...])
@@ -116,21 +112,21 @@
         return pltpu.make_async_remote_copy(
             src_ref=rsend.at[c, dest, pl.ds(0, capacity)],
             dst_ref=rrecv.at[c, source, pl.ds(0, capacity)],
-            send_sem=rs.at[c, dest], recv_sem=rr.at[c, source],
+            send_sem=rs, recv_sem=rr.at[c],
             device_id=(dest, place), device_id_type=MESH,
         )
 
     def meta_copy(dest, source):
         return pltpu.make_async_remote_copy(
             src_ref=msend.at[dest], dst_ref=mrecv.at[source],
-            send_sem=ms.at[dest], recv_sem=mr.at[source],
+            send_sem=ms, recv_sem=mr,
             device_id=(dest, place), device_id_type=MESH,
         )
 
     def score_copy(dest, source):
         return pltpu.make_async_remote_copy(
             src_ref=tsend.at[dest], dst_ref=trecv.at[source],
-            send_sem=ts.at[dest], recv_sem=tr.at[source],
+            send_sem=ts, recv_sem=tr,
             device_id=(dest, place), device_id_type=MESH,
         )
 
@@ -156,6 +152,16 @@
         )
 
     fill(0)
+    pl.semaphore_wait(barrier, window - 1 + chips)
+
+    def launch_weights(c, carry):
+        for step in range(1, chips):
+            weight_copy(c, across(step), step, place).start()
+        weight_copy(c, mate, 0, place).start()
+        return carry
+
+    lax.fori_loop(0, pieces, launch_weights, 0)
+
     for step in range(1, window):
         meta_copy(other(step), me).start()
 
@@ -187,21 +193,28 @@
     for keep in keeps:
         keep.wait()
 
-    for step in range(1, window):
-        meta_copy(other(step), lax.rem(me + window - step, window)).wait_recv()
+    settle(mrecv, mr)
     for s in range(window):
         gates[s] = jnp.sum(
             jnp.where(spread(mrecv, s), mrecv[s, 1:2, :], 0.0), axis=1, keepdims=True
         )
 
+    def combine(c):
+        lanes = pl.ds(pl.multiple_of(c * piece, piece), piece)
+        core_copy(c).wait_recv()
+        for step in range(1, chips):
+            to = chip_at(step)
+            ysend[c, step] = (own[c, to] + crecv[c, to].astype(jnp.float32)).astype(jnp.bfloat16)
+            sum_copy(c, step).start()
+        down_ref[:, lanes] = own[c, chip] + crecv[c, chip].astype(jnp.float32)
+
     def finish(c, carry):
-        lanes = pl.ds(pl.multiple_of(c * piece, piece), piece)
         for step in range(1, chips):
             came = lax.rem(chip + chips - step, chips) * 2 + core
             weight_copy(c, across(step), step, came).wait_recv()
             pass_copy(c, step, came).start()
-        for step in range(1, window):
-            row_copy(c, other(step), lax.rem(me + window - step, window)).wait_recv()
+        came_rows = rrecv.at[c, pl.ds(0, window - 1), pl.ds(0, capacity)]
+        pltpu.make_async_copy(came_rows, came_rows, rr.at[c]).wait()
         got = rrecv[c].reshape(slots_all, piece)
         scaled = (gates[...].reshape(slots_all, 1) * got.astype(jnp.float32)).astype(jnp.bfloat16)
         for h in range(chips):
@@ -210,7 +223,7 @@
             ).astype(jnp.bfloat16)
         core_copy(c).start()
         for h in range(chips):
-            own[h] = jnp.dot(hturn[2 * h + core], scaled, preferred_element_type=jnp.float32)
+            own[c, h] = jnp.dot(hturn[2 * h + core], scaled, preferred_element_type=jnp.float32)
         weight_copy(c, mate, 0, chip * 2 + 1 - core).wait_recv()
         for step in range(1, chips):
             came = lax.rem(chip + chips - step, chips) * 2 + 1 - core
@@ -219,15 +232,15 @@
         upward[...] += lax.dot_general(
             got, weights, (((1,), (1,)), ((), ())), preferred_element_type=jnp.float32
         )
-        core_copy(c).wait_recv()
-        for step in range(1, chips):
-            to = chip_at(step)
-            ysend[c, step] = (own[to] + crecv[c, to].astype(jnp.float32)).astype(jnp.bfloat16)
-            sum_copy(c, step).start()
-        down_ref[:, lanes] = own[chip] + crecv[c, chip].astype(jnp.float32)
+
+        @pl.when(c > 0)
+        def _():
+            combine(c - 1)
+
         return carry
 
     lax.fori_loop(0, pieces, finish, 0)
+    combine(pieces - 1)
 
     for s in range(window):
         up = upward[s * rows : (s + 1) * rows]
@@ -241,39 +254,40 @@
         up = upward[s * rows : s * rows + capacity]
         gradh_ref[s] = (gates[s, 0:capacity] * up).astype(jnp.bfloat16)
 
-    for step in range(1, window):
-        score_copy(other(step), lax.rem(me + window - step, window)).wait_recv()
+    def collect(c, carry):
+        lanes = pl.ds(pl.multiple_of(c * piece, piece), piece)
+        for step in range(1, chips):
+            sum_copy(c, step).wait_recv()
+            down_ref[:, lanes] += yrecv[c, step].astype(jnp.float32)
+        return carry
+
+    def drain(c, carry):
+        for step in range(1, chips):
+            weight_copy(c, across(step), step, place).wait_send()
+            pass_copy(c, step, lax.rem(chip + chips - step, chips) * 2 + core).wait_send()
+        weight_copy(c, mate, 0, place).wait_send()
+        core_copy(c).wait_send()
+        return carry
+
+    lax.fori_loop(0, pieces, drain, 0)
+    sent_rows = rsend.at[:, pl.ds(0, window - 1), pl.ds(0, capacity)]
+    pltpu.make_async_copy(sent_rows, sent_rows, rs).wait()
+    settle(msend, ms)
+    lax.fori_loop(0, pieces - 1, collect, 0)
+
+    settle(trecv, tr)
     token_scores = jnp.zeros((k, tokens), jnp.float32)
     for w in range(window):
         token_scores = jnp.where(chosen == w, trecv[w], token_scores)
     scores_all = jnp.where(live, token_scores, outside)
     mean_score = jnp.sum(gating * scores_all, axis=0, keepdims=True)
     logit_ref[...] = gating * (scores_all - mean_score)
-
-    def collect(c, carry):
-        lanes = pl.ds(pl.multiple_of(c * piece, piece), piece)
-        for step in range(1, chips):
-            sum_copy(c, step).wait_recv()
-            down_ref[:, lanes] += yrecv[c, step].astype(jnp.float32)
-        return carry
-
-    lax.fori_loop(0, pieces, collect, 0)
-
-    def drain(c, carry):
-        for step in range(1, window):
-            row_copy(c, other(step), me).wait_send()
-        for step in range(1, chips):
-            weight_copy(c, across(step), step, place).wait_send()
-            pass_copy(c, step, lax.rem(chip + chips - step, chips) * 2 + core).wait_send()
+    settle(tsend, ts)
+
+    collect(pieces - 1, 0)
+    for c in range(pieces):
+        for step in range(1, chips):
             sum_copy(c, step).wait_send()
-        weight_copy(c, mate, 0, place).wait_send()
-        core_copy(c).wait_send()
-        return carry
-
-    lax.fori_loop(0, pieces, drain, 0)
-    for step in range(1, window):
-        meta_copy(other(step), me).wait_send()
-        score_copy(other(step), me).wait_send()
 
 
 def write_out(a, b, c, a_out, b_out, c_out, sems):
@@ -325,7 +339,7 @@
             pltpu.VMEM((window, rows, hidden_units), bf),
             pltpu.VMEM((shards, shard_rows, slots_all), bf),
             pltpu.VMEM((slots_all, hidden_units), f32),
-            pltpu.VMEM((chips, shard_rows, piece), f32),
+            pltpu.VMEM((PIECES, chips, shard_rows, piece), f32),
             pltpu.VMEM((PIECES, chips, shard_rows, piece), bf),
             pltpu.VMEM((PIECES, chips, shard_rows, piece), bf),
             pltpu.VMEM((PIECES, chips, shard_rows, piece), bf),
@@ -333,13 +347,13 @@
             pltpu.VMEM((window, 8, tokens), f32),
             pltpu.VMEM((window, 8, tokens), f32),
             pltpu.VMEM((window, rows, 1), f32),
-            dma((PIECES, window)), dma((PIECES, window)),
-            dma((window,)), dma((window,)),
+            dma, dma((PIECES,)),
+            dma, dma,
             dma((PIECES, chips)), dma((PIECES, chips)),
             dma((PIECES, chips)), dma((PIECES, chips)),
             dma((PIECES,)), dma((PIECES,)),
             dma((PIECES, chips)), dma((PIECES, chips)),
-            dma((window,)), dma((window,)),
+            dma, dma,
             dma((6,)), dma((PIECES,)),
         ],
         compiler_params=pltpu.CompilerParams(

time: 48.9 us -> 47.4 us (0.969)
  Pallas kernels: 48.1 us -> 46.6 us
    pallas_call x1, Pallas kernels: 46.8 us -> 45.3 us  [fused(): pl.pallas_call(functools.partial(kernel, window, shards, capacity, PIECES...]
where the time goes in v3:
time: 47.4 us; the launch traced here: 47.2 us
  Pallas kernels  46.6 us (98%)
  between operations  0.64 us (1%)
    pallas_call x1, Pallas kernels, fused(): pl.pallas_call(functools.partial(kernel, window, shards, capacity, PIECES...  45.3 us
    pallas_call x1, Pallas kernels, fused(): pl.pallas_call(write_out, out_shape=tuple((jax.ShapeDtypeStruct(a.shape,...  1.33 us

profile of v3, /device:TPU:0, one launch (start us, length us, event | category | flops | bytes accessed | tf_op | source)
XLA Modules:
  0.0 47.2 jit_solution(12415989593689603870)
XLA Ops:
  0.6 45.3 %shard_map.94 = (bf16[8,40,768]{2,1,0:T(8,128)(2,1)S(1)}, f32[192,2048]{1,0:T(8,128)S(1)}, f32[8,128]{1,0:T(8,128)S(1)}) custom-call(bf16[128,2048]{1,0:T(8,128)(2,1)} %token_hbm.1, f32[8,128]{1,0:T(8,128)} %bitcast.11, s32[8,128]{1,0:T(8,128)} %bitcast.12, s32[8,128]{1,0:T(8,128)} %bitcast.13, f32[8,128]{1,0:T(8,128)} %bitcast.14, ...), custom_call_target="tpu_custom_call" | custom-call | tf_op jit(solution)/shard_map/pallas_call | solution.py:318
  45.9 1.3 %shard_map.95 = (bf16[8,40,768]{2,1,0:T(8,128)(2,1)}, f32[192,2048]{1,0:T(8,128)}, f32[8,128]{1,0:T(8,128)}) custom-call(bf16[8,40,768]{2,1,0:T(8,128)(2,1)S(1)} %get-tuple-element.9.a, f32[192,2048]{1,0:T(8,128)S(1)} %get-tuple-element.10.b, f32[8,128]{1,0:T(8,128)S(1)} %get-tuple-element.11.c), custom_call_target="tpu_custom_call" | custom-call | tf_op jit(solution)/shard_map/pallas_call | solution.py:369
